TPU v7x, 32 devices: a 4x4x1 block of a 4x4x8 slice. The times are simulated.
32 devices in a mesh: dp: 1 (over z), ep: 4 (over y), tp: 8 (over x, core).
Axes of the slice: x: 4, y: 4, z: 1, core: 2. Of those that a mesh axis runs over, the one named last changes fastest.
The devices are a block of a 4x4x8 slice.
Arguments:
- X: bfloat16 [4096, 2048], P(('dp', 'ep', 'tp'))
- idx: int32 [4096, 8], P(('dp', 'ep', 'tp'))
- g: float32 [4096, 8], P(('dp', 'ep', 'tp'))
- W1: bfloat16 [64, 2048, 1024], P('ep', None, 'tp')
- W3: bfloat16 [64, 2048, 1024], P('ep', None, 'tp')
- W2: bfloat16 [64, 1024, 2048], P('ep', 'tp')
Outputs:
- output: bfloat16 [4096, 2048], P(('dp', 'ep', 'tp'))
All inputs are finite; a program needn't handle non-finite values.
Results may differ from a plain program's by a relative error of at most 0.0100285.
Values are sent between devices in bfloat16 or wider.
A program may use at most 768 MiB of HBM per device.

v0:
```python
import jax
import jax.numpy as jnp
from jax import lax
from jax.sharding import PartitionSpec as P

CF = 2


def _route(idx, n_exp, cap):
    ids = idx.reshape(-1)
    oh = (ids[:, None] == jnp.arange(n_exp, dtype=jnp.int32)[None, :]).astype(jnp.int32)
    s = jnp.sum(oh * (jnp.cumsum(oh, axis=0) - 1), axis=1)
    keep = s < cap
    return jnp.where(keep, ids * cap + s, n_exp * cap), keep


def solution(mesh):
    ep, tp = mesh.shape["ep"], mesh.shape["tp"]
    rows = P(("dp", "ep", "tp"), None)

    def local(x, idx, g, w1, w3, w2):
        t_loc, d = x.shape
        top = idx.shape[1]
        el = w1.shape[0]
        n_exp = el * ep
        cap = CF * top * t_loc // n_exp
        dest, keep = _route(idx, n_exp, cap)
        xr = jnp.repeat(x, top, axis=0)
        buf = jnp.zeros((n_exp * cap, d), x.dtype).at[dest].set(xr, mode="drop").reshape(ep, el, cap, d)
        recv = lax.all_to_all(buf, "ep", 0, 0, tiled=True)
        allr = lax.all_gather(recv, "tp", axis=0)
        xe = allr.transpose(2, 0, 1, 3, 4).reshape(el, tp * ep * cap, d)
        h1 = jnp.einsum("erd,edf->erf", xe, w1, preferred_element_type=jnp.float32)
        h3 = jnp.einsum("erd,edf->erf", xe, w3, preferred_element_type=jnp.float32)
        h = (jax.nn.silu(h1) * h3).astype(jnp.bfloat16)
        yp = jnp.einsum("erf,efd->erd", h, w2, preferred_element_type=jnp.float32).astype(jnp.bfloat16)
        yp = yp.reshape(el, tp, ep, cap, d).transpose(1, 2, 0, 3, 4)
        parts = lax.all_to_all(yp, "tp", 0, 0, tiled=True)
        y = jnp.sum(parts.astype(jnp.float32), axis=0).astype(jnp.bfloat16)
        back = lax.all_to_all(y, "ep", 0, 0, tiled=True).reshape(n_exp * cap, d)
        ysel = back[jnp.minimum(dest, n_exp * cap - 1)].astype(jnp.float32).reshape(t_loc, top, d)
        wgt = jnp.where(keep, g.reshape(-1), 0.0).reshape(t_loc, top, 1)
        return jnp.sum(ysel * wgt, axis=1).astype(jnp.bfloat16)

    return jax.shard_map(local, mesh=mesh,
                         in_specs=(rows, rows, rows, P("ep", None, "tp"), P("ep", None, "tp"), P("ep", "tp", None)),
                         out_specs=rows, check_vma=False)
```

profile of v0, /device:TPU:97, one launch (start us, length us, event | category | flops | bytes accessed | tf_op | source)
XLA Modules:
  0.0 1519.5 jit_solution(15687841426906021441)
XLA Ops:
  6.5 0.0 copy-start
  6.6 0.0 all-gather.3.cloned.1.call-start
  6.6 0.8 copy.25
  7.4 0.1 eq.29
  7.5 0.1 eq.25
  7.6 0.7 broadcast_multiply_fusion
  8.3 18.0 %reduce-window.6 = s32[64,8,128]{2,1,0:T(8,128)S(1)} reduce-window(s32[64,8,128]{2,1,0:T(8,128)S(1)} %fusion.8, s32[]{:T(128)} %constant.9.clone.1), window={size=1x1x128 pad=0_0x0_0x127_0}, to_apply=%region_0.0 | reduce-window | flops 8323072 | bytes 524292 | tf_op jit(solution)/shard_map/reduce-window
  26.3 0.1 slice.10
  26.4 0.1 copy.27
  26.6 0.1 copy.28
  26.7 0.1 add_add_fusion
  26.9 0.1 copy.29
  27.0 0.1 mul.37
  27.1 0.1 fusion.7
  27.1 0.0 copy-start.2
  27.1 0.6 copy-done.2
  27.7 0.6 compare_select_fusion
  28.3 0.0 copy-done
  28.3 11.2 scatter_custom_fusion
  39.6 103.1 %all_to_all.15 = bf16[4,16,32,2048]{3,2,1,0:T(8,128)(2,1)} all-to-all(bf16[4,16,32,2048]{3,2,1,0:T(8,128)(2,1)} %bitcast.51), channel_id=1, replica_groups=mesh['dp'=1,'ep'=4,'tp'=8] {'ep'}, dimensions={0} | all-to-all | bytes 16777216 | tf_op jit(solution)/shard_map/all_to_all | solution.py:30
  142.7 0.1 all-gather.3.cloned.1.call-update
  142.7 295.5 %all-gather.3.cloned.1.call-done = bf16[32,16,32,2048]{3,2,1,0:T(8,128)(2,1)} async-done(((bf16[4,16,32,2048]{3,2,1,0:T(8,128)(2,1)}), bf16[32,16,32,2048]{3,2,1,0:T(8,128)(2,1)}) %all-gather.3.cloned.1.call-update) | async-done | bytes 67108880 | tf_op jit(solution)/shard_map/all_gather | solution.py:31
  438.3 44.1 %copy.30 = bf16[8,4,16,32,2048]{4,3,1,0,2:T(8,128)(2,1)} copy(bf16[8,4,16,32,2048]{4,3,2,1,0:T(8,128)(2,1)} %bitcast.6) | data formatting | bytes 134217728 | tf_op jit(solution)/shard_map/all_gather | solution.py:31
  482.3 30.9 %fusion.10 = f32[16,1024,128]{2,1,0:T(8,128)} fusion(bf16[16,1024,2048]{2,1,0:T(8,128)(2,1)} %bitcast.8, bf16[16,2048,128]{2,1,0:T(8,128)(2,1)} %param.9), kind=kOutput, calls=%fused_computation.27 | convolution fusion | flops 8589934592 | bytes 83886080 | tf_op jit(solution)/shard_map/erd,edf->erf/dot_general | solution.py:33
  513.2 60.9 %convolution_convert_fusion = bf16[16,1024,2048]{2,1,0:T(8,128)(2,1)} fusion(bf16[16,128,2048]{2,1,0:T(8,128)(2,1)} %param.11, f32[16,1024,128]{2,1,0:T(8,128)} %fusion.10, bf16[16,1024,2048]{2,1,0:T(8,128)(2,1)} %bitcast.8, bf16[16,2048,128]{2,1,0:T(8,128)(2,1)} %param.10), kind=kOutput, calls=%fused_computation.3 | convolution fusion | flops 17226006528 | bytes 159383552 | tf_op jit(solution)/shard_map/erf,efd->erd/dot_general | solution.py:36
  574.1 44.1 %copy.39 = bf16[16,8,4,32,2048]{4,3,2,0,1:T(8,128)(2,1)} copy(bf16[16,8,4,32,2048]{4,3,2,1,0:T(8,128)(2,1)} %bitcast.10) | data formatting | bytes 134217728 | tf_op jit(solution)/shard_map/reshape | solution.py:37
  618.2 741.1 %all_to_all.16 = bf16[8,4,16,32,2048]{4,3,1,2,0:T(8,128)(2,1)} all-to-all(bf16[8,4,16,32,2048]{4,3,1,2,0:T(8,128)(2,1)} %bitcast.50), channel_id=1, replica_groups=mesh['dp'=1,'ep'=4,'tp'=8] {'tp'}, dimensions={0} | all-to-all | bytes 134217728 | tf_op jit(solution)/shard_map/all_to_all | solution.py:38
  1359.3 25.9 %reduce_sum.34 = bf16[4,16,32,2048]{3,2,0,1:T(8,128)(2,1)} reduce(bf16[8,4,16,32,2048]{4,3,1,2,0:T(8,128)(2,1)} %all_to_all.16, bf16[]{:T(256)} %constant.8.clone.1), dimensions={0}, to_apply=%region_4.5 | reduce | flops 29360128 | bytes 75497472 | tf_op jit(solution)/shard_map/reduce_sum | solution.py:39
  1385.2 8.3 copy.33
  1393.5 0.0 copy-start.3
  1393.5 0.0 copy-start.5
  1393.5 0.0 copy-start.4
  1393.5 5.9 all-to-all-start.2
  1399.4 0.0 copy-done.3
  1399.4 0.1 lt.45
  1399.5 0.0 copy-done.5
  1399.5 0.1 copy.34
  1399.6 0.0 copy-done.4
  1399.6 92.3 %all-to-all-done.2 = bf16[4,16,32,2048]{3,2,1,0:T(8,128)(2,1)} async-done(((bf16[4,16,32,2048]{3,2,1,0:T(8,128)(2,1)}), bf16[4,16,32,2048]{3,2,1,0:T(8,128)(2,1)}, u32[]{:S(2)}, u32[]{:S(2)}) %all-to-all-start.2) | async-done | bytes 8388640 | tf_op jit(solution)/shard_map/all_to_all | solution.py:40
  1492.0 0.0 copy-start.1
  1492.0 13.3 gather_fusion
  1505.3 7.3 fusion
  1512.6 0.0 copy-done.1
  (7 shorter events, 0.1 us)
Async XLA Ops:
  6.5 21.8 %copy-start = (bf16[128,2048]{1,0:T(8,128)(2,1)S(1)}, bf16[128,2048]{1,0:T(8,128)(2,1)}, u32[]{:S(2)}) copy-start(bf16[128,2048]{1,0:T(8,128)(2,1)} %param.6) | copy-start | bytes 1572868
  6.6 431.7 %all-gather.3.cloned.1.call-start = ((), (), s32[]{:S(2)}) async-start(), calls=%async_computation.3 | async-start | bytes 75497472 | tf_op jit(solution)/shard_map/all_gather | solution.py:31
  27.1 0.6 copy-start.2
  1393.5 5.9 copy-start.3
  1393.5 6.0 copy-start.5
  1393.5 6.1 copy-start.4
  1393.5 98.5 %all-to-all-start.2 = ((bf16[4,16,32,2048]{3,2,1,0:T(8,128)(2,1)}), bf16[4,16,32,2048]{3,2,1,0:T(8,128)(2,1)}, u32[]{:S(2)}, u32[]{:S(2)}) async-start(bf16[4,16,32,2048]{3,2,1,0:T(8,128)(2,1)} %copy.33), calls=%async_computation.2 | async-start | bytes 16777216 | tf_op jit(solution)/shard_map/all_to_all | solution.py:40
  1492.0 20.7 %copy-start.1 = (bf16[128,2048]{1,0:T(8,128)(2,1)S(1)}, bf16[128,2048]{1,0:T(8,128)(2,1)}, u32[]{:S(2)}) copy-start(bf16[128,2048]{1,0:T(8,128)(2,1)} %param.6) | copy-start | bytes 1572868
Sparse Core Ops, SparseCore 0:
  142.9 295.3 all-gather.2
where the time goes:
time: 1520 us
  blocking collectives  844 us (56%)
  waiting for transfers between devices  388 us (26%)
  local copies, waits for them, and re-layouts  123 us (8%)
  matrix products  91.8 us (6%)
  other arithmetic  52.8 us (3%)
    all_to_all x1, blocking collectives, local(): parts = lax.all_to_all(yp, 'tp', 0, 0, tiled=True)  741 us
    all_gather x1, waiting for transfers between devices, local(): allr = lax.all_gather(recv, 'tp', axis=0)  296 us
    all_to_all x1, blocking collectives, local(): recv = lax.all_to_all(buf, 'ep', 0, 0, tiled=True)  103 us
    all_to_all x1, waiting for transfers between devices, local(): back = lax.all_to_all(y, 'ep', 0, 0, tiled=True).reshape(n_exp * cap, d)  92.3 us
    dot_general x1, matrix products, local(): jnp.einsum('erf,efd->erd', h, w2, preferred_element_type=jnp.float32)  60.9 us
    all_gather x1, local copies, waits for them, and re-layouts, local(): allr = lax.all_gather(recv, 'tp', axis=0)  44.1 us
    reshape x1, local copies, waits for them, and re-layouts, local(): yp = yp.reshape(el, tp, ep, cap, d).transpose(1, 2, 0, 3, 4)  44.1 us
    dot_general x1, matrix products, local(): h1 = jnp.einsum('erd,edf->erf', xe, w1, preferred_element_type=jnp.float32)  30.9 us
  transfers between devices with their start and end apart: 2, of which 2 were waited for; matrix products, arithmetic and copies ran while one was open for 0% of the time, Pallas kernels for 0%

commit v1 on v0

v1 whole, which is shorter than its diff:
```python
import functools

import jax
import jax.numpy as jnp
from jax import lax
from jax.experimental import pallas as pl
from jax.experimental.pallas import tpu as pltpu
from jax.sharding import PartitionSpec as P

CF = 2
RING = 4
MESH = pl.DeviceIdType.MESH
F32, BF16 = jnp.float32, jnp.bfloat16
VMEM_LIMIT = 66 * 1000 * 1000


def _neighbours():
    d, y, t = lax.axis_index("dp"), lax.axis_index("ep"), lax.axis_index("tp")
    x, c = t // 2, t % 2

    def at(dx, dy):
        return (d, (y + dy) % RING, 2 * ((x + dx) % RING) + c)

    pr, pl_ = at(1 - c, c), at(RING - 1 + c, RING - c)
    qr, ql = at(c, 1 - c), at(RING - c, RING - 1 + c)
    return pr, pl_, qr, ql, (d, y, 2 * x + 1 - c)


def _greet(devices):
    barrier = pltpu.get_barrier_semaphore()
    for dev in devices:
        pl.semaphore_signal(barrier, inc=1, device_id=dev, device_id_type=MESH)
    pl.semaphore_wait(barrier, len(devices))


def _up(cap, x, meta, w1, w3, w2, h_out, sg_out, w2x, A, MA, Wt, G, Hb, SG, ssem, rsem, lsem):
    pr, pl_, qr, ql, mate = _neighbours()
    el = w1.shape[0]
    t_loc, d = x.shape
    hf = t_loc // 2
    lo, hi = pl.ds(0, hf), pl.ds(hf, hf)
    gs = el // 4
    fw = w1.shape[2]
    count = [0]

    def remote(src, dst, dev):
        i = count[0]
        count[0] += 1
        return pltpu.make_async_remote_copy(src_ref=src, dst_ref=dst, send_sem=ssem.at[i], recv_sem=rsem.at[i],
                                            device_id=dev, device_id_type=MESH)

    sent = []

    def go(*copies):
        for cp in copies:
            cp.start()
            sent.append(cp)

    lcount = [0]

    def local(src, dst):
        i = lcount[0]
        lcount[0] += 1
        cp = pltpu.make_async_copy(src, dst, lsem.at[i])
        cp.start()
        return cp

    _greet((pr, pl_, qr, ql, mate))

    own_x = local(x, A.at[0, 0])
    own_m = local(meta, MA.at[0, 0])
    r_m, l_m = remote(meta, MA.at[0, 3], pr), remote(meta, MA.at[0, 1], pl_)
    r_lo, r_hi = remote(x.at[lo], A.at[0, 3, lo], pr), remote(x.at[hi], A.at[0, 3, hi], pr)
    l_hi, l_lo = remote(x.at[hi], A.at[0, 1, hi], pl_), remote(x.at[lo], A.at[0, 1, lo], pl_)
    go(r_m, l_m, r_lo, l_hi, r_hi, l_lo)

    own_w, mate_w = [], []
    for g in range(4):
        es = pl.ds(g * gs, gs)
        own_w.append((local(w1.at[es], Wt.at[es, 0, :, pl.ds(0, fw)]), local(w3.at[es], Wt.at[es, 0, :, pl.ds(fw, fw)])))
    for g in range(4):
        es = pl.ds(g * gs, gs)
        pair = (remote(w1.at[es], Wt.at[es, 1, :, pl.ds(0, fw)], mate), remote(w3.at[es], Wt.at[es, 1, :, pl.ds(fw, fw)], mate))
        go(*pair)
        mate_w.append(pair)
    w2_cp = remote(w2, w2x, mate)
    go(w2_cp)

    f_lo, f_hi = remote(A.at[0, 3, lo], A.at[0, 2, lo], pr), remote(A.at[0, 1, hi], A.at[0, 2, hi], pl_)
    f_m = remote(MA.at[0, 3], MA.at[0, 2], pr)
    r_m.wait_recv()
    go(f_m)
    r_lo.wait_recv()
    go(f_lo)
    l_hi.wait_recv()
    go(f_hi)

    qR = [remote(x if i == 0 else A.at[0, i], A.at[3, i], qr) for i in range(4)]
    qL = [remote(x if i == 0 else A.at[0, i], A.at[1, i], ql) for i in range(4)]
    fR = [remote(A.at[3, i, lo], A.at[2, i, lo], qr) for i in range(4)]
    fL = [remote(A.at[1, i, hi], A.at[2, i, hi], ql) for i in range(4)]
    mR, mL, mF = remote(MA.at[0], MA.at[3], qr), remote(MA.at[0], MA.at[1], ql), remote(MA.at[3], MA.at[2], qr)

    go(qR[0], qL[0])
    l_m.wait_recv()
    l_lo.wait_recv()
    go(qR[1], qL[1])
    r_hi.wait_recv()
    go(qR[3], qL[3])
    f_m.wait_recv()
    own_m.wait()
    go(mR, mL)
    f_lo.wait_recv()
    f_hi.wait_recv()
    go(qR[2], qL[2])
    own_x.wait()

    first = (lax.axis_index("ep") * el).astype(F32)
    eid = lax.broadcasted_iota(jnp.int32, (el, t_loc), 0).astype(F32) + first
    tri = (lax.broadcasted_iota(jnp.int32, (t_loc, t_loc), 0)
           < lax.broadcasted_iota(jnp.int32, (t_loc, t_loc), 1)).astype(F32).astype(BF16)
    slot_no = lax.broadcasted_iota(jnp.int32, (cap, t_loc), 0).astype(F32)
    top = meta.shape[0] // 2

    def gather(block):
        def body(i, _):
            b = block(i)
            m = MA.at[b // 4, b % 4]
            hold = jnp.zeros((el, t_loc), F32)
            gate = jnp.zeros((el, t_loc), F32)
            for j in range(top):
                hit = jnp.broadcast_to(m[j:j + 1, :], (el, t_loc)) == eid
                hold = hold + jnp.where(hit, 1.0, 0.0)
                gate = gate + jnp.where(hit, jnp.broadcast_to(m[top + j:top + j + 1, :], (el, t_loc)), 0.0)
            slot = jnp.dot(hold.astype(BF16), tri, preferred_element_type=F32)
            keep = (hold > 0.5) & (slot < cap)
            slot = jnp.where(keep, slot, -1.0)
            SG[b, 0:el, :] = slot
            SG[b, el:2 * el, :] = jnp.where(keep, gate, 0.0)
            pick = jnp.concatenate(
                [jnp.where(jnp.broadcast_to(slot[e:e + 1, :], (cap, t_loc)) == slot_no, 1.0, 0.0) for e in range(el)], axis=0
            ).astype(BF16)
            at = pl.ds(pl.multiple_of(i * cap, cap), cap)
            for n in range(d // 256):
                cols = pl.ds(n * 256, 256)
                rows = jnp.dot(pick, A[b // 4, b % 4, :, cols], preferred_element_type=F32).astype(BF16)
                G[:, at, cols] = rows.reshape(el, cap, 256)
            return 0
        lax.fori_loop(0, 4, body, 0)

    def up(e0, e1, s, blocks):
        def one(e):
            o = jnp.dot(G[e], Wt[e, s], preferred_element_type=F32)
            a, b = o[:, :fw], o[:, fw:]
            h = (jax.nn.silu(a) * b).astype(BF16)
            for i, (dq, dp) in enumerate(blocks):
                Hb[dp, e, dq * cap:(dq + 1) * cap, s * fw:(s + 1) * fw] = h[i * cap:(i + 1) * cap]

        def body(k, _):
            for u in range(4):
                one(e0 + k * 4 + u)
            return 0
        lax.fori_loop(0, (e1 - e0) // 4, body, 0)

    gather(lambda i: i)
    blocks = [(0, i) for i in range(4)]
    for g in range(4):
        for cp in own_w[g]:
            cp.wait()
    up(0, el, 0, blocks)
    for g in range(4):
        for cp in mate_w[g]:
            cp.wait_recv()
        up(g * gs, (g + 1) * gs, 1, blocks)

    mR.wait_recv()
    go(mF)
    mL.wait_recv()
    for i in (0, 1):
        qR[i].wait_recv()
        qL[i].wait_recv()
        go(fR[i], fL[i])
    gather(lambda i: 12 - 8 * (i // 2) + i % 2)
    blocks = [(3, 0), (3, 1), (1, 0), (1, 1)]
    up(0, el, 0, blocks)
    up(0, el, 1, blocks)

    for i in (3, 2):
        qR[i].wait_recv()
        qL[i].wait_recv()
        go(fR[i], fL[i])
    gather(lambda i: 14 - 8 * (i // 2) + i % 2)
    blocks = [(3, 2), (3, 3), (1, 2), (1, 3)]
    up(0, el, 0, blocks)
    up(0, el, 1, blocks)

    mF.wait_recv()
    for i in range(4):
        fR[i].wait_recv()
        fL[i].wait_recv()
    gather(lambda i: 8 + i)
    sg_cp = local(SG, sg_out)
    blocks = [(2, i) for i in range(4)]
    up(0, el, 0, blocks)
    up(0, el, 1, blocks)
    h_cp = local(Hb, h_out)
    w2_cp.wait_recv()
    for cp in sent:
        cp.wait_send()
    sg_cp.wait()
    h_cp.wait()


def _down(cap, h_in, sg_in, w2, w2x, o_ref, W2f, Hv, YP, SG, C3, sF, sR, sL, S0, K1, K3, FR, FL, RL, RR,
          bF, bR, bL, T0, T1, T3, bFR, bFL, bRL, bRR, ssem, rsem, lsem):
    pr, pl_, qr, ql, mate = _neighbours()
    el, fw, d = w2.shape
    t_loc = o_ref.shape[0]
    hf = t_loc // 2
    lo, hi = pl.ds(0, hf), pl.ds(hf, hf)
    gs = el // 4
    count, lcount = [0], [0]
    sent = []

    def remote(src, dst, dev):
        i = count[0]
        count[0] += 1
        return pltpu.make_async_remote_copy(src_ref=src, dst_ref=dst, send_sem=ssem.at[i], recv_sem=rsem.at[i],
                                            device_id=dev, device_id_type=MESH)

    def go(*copies):
        for cp in copies:
            cp.start()
            sent.append(cp)

    def local(src, dst):
        i = lcount[0]
        lcount[0] += 1
        cp = pltpu.make_async_copy(src, dst, lsem.at[i])
        cp.start()
        return cp

    order = (2, 1, 3, 0)
    sg_cp = local(sg_in, SG)
    h_cp = {order[0]: local(h_in.at[order[0]], Hv.at[order[0]])}
    w_cp = []
    for g in range(4):
        es = pl.ds(g * gs, gs)
        w_cp.append((local(w2.at[es], W2f.at[es, pl.ds(0, fw)]), local(w2x.at[es], W2f.at[es, pl.ds(fw, fw)])))
    for dp in order[1:]:
        h_cp[dp] = local(h_in.at[dp], Hv.at[dp])
    _greet((pr, pl_, qr, ql, mate))

    far_r = [remote(sF.at[i, lo], FR.at[i], qr) for i in range(4)]
    far_l = [remote(sF.at[i, hi], FL.at[i], ql) for i in range(4)]
    near_r = [(remote(sR.at[i, lo], RL.at[i, lo], qr), remote(sR.at[i, hi], RL.at[i, hi], qr)) for i in range(4)]
    near_l = [(remote(sL.at[i, lo], RR.at[i, lo], ql), remote(sL.at[i, hi], RR.at[i, hi], ql)) for i in range(4)]
    b_far_r, b_far_l = remote(bF.at[lo], bFR, pr), remote(bF.at[hi], bFL, pl_)
    b_near_r = (remote(bR.at[lo], bRL.at[lo], pr), remote(bR.at[hi], bRL.at[hi], pr))
    b_near_l = (remote(bL.at[lo], bRR.at[lo], pl_), remote(bL.at[hi], bRR.at[hi], pl_))

    ncol = el * cap
    row_no = lax.broadcasted_iota(jnp.int32, (4 * el, ncol), 0)
    col_e = lax.broadcasted_iota(jnp.int32, (4 * el, ncol), 1) // cap
    spread = [jnp.where(row_no == col_e + k * el, 1.0, 0.0).astype(BF16) for k in range(4)]
    col_s = (lax.broadcasted_iota(jnp.int32, (t_loc, ncol), 1) % cap).astype(F32)

    def down(dp, e0, e1):
        def one(e):
            for n in range(d // 256):
                cols = pl.ds(n * 256, 256)
                y = jnp.dot(Hv[dp, e], W2f[e, :, cols], preferred_element_type=F32).astype(BF16)
                YP[:, pl.ds(pl.multiple_of(e * cap, cap), cap), cols] = y.reshape(4, cap, 256)

        def body(k, _):
            for u in range(2):
                one(e0 + k * 2 + u)
            return 0
        lax.fori_loop(0, (e1 - e0) // 2, body, 0)

    def combine(dp, dq, put):
        b = dq * 4 + dp
        gate = SG[b, el:2 * el, :]
        g1 = gate.astype(BF16).astype(F32)
        g2 = (gate - g1).astype(BF16).astype(F32)
        g3 = gate - g1 - g2
        table = jnp.concatenate([SG[b, 0:el, :], g1, g2, g3], axis=0).T.astype(BF16)
        slot = jnp.dot(table, spread[0], preferred_element_type=F32)
        hit = slot == col_s
        for k in range(3):
            piece = jnp.dot(table, spread[k + 1], preferred_element_type=F32)
            C3[k * t_loc:(k + 1) * t_loc, :] = jnp.where(hit, piece, 0.0).astype(BF16)
        for n in range(d // 256):
            cols = pl.ds(n * 256, 256)
            z = jnp.dot(C3[...], YP[dq, :, cols], preferred_element_type=F32)
            put(z[:t_loc] + z[t_loc:2 * t_loc] + z[2 * t_loc:], cols)

    def put_far(dp):
        def put(z, cols):
            sF[dp, :, cols] = z.astype(BF16)
        return put

    def put_right(dp):
        def put(z, cols):
            K1[dp, :, cols] = z[:hf]
            sR[dp, hi, cols] = z[hf:].astype(BF16)
        return put

    def put_left(dp):
        def put(z, cols):
            K3[dp, :, cols] = z[hf:]
            sL[dp, lo, cols] = z[:hf].astype(BF16)
        return put

    def put_own(dp):
        def put(z, cols):
            S0[dp, :, cols] = z
        return put

    def pass_on(dp):
        far_r[dp].wait_recv()
        sR[dp, lo, :] = (K1[dp] + FR[dp].astype(F32)).astype(BF16)
        go(near_r[dp][0])
        far_l[dp].wait_recv()
        sL[dp, hi, :] = (K3[dp] + FL[dp].astype(F32)).astype(BF16)
        go(near_l[dp][1])

    def finish(dp):
        for cp in near_r[dp] + near_l[dp]:
            cp.wait_recv()

        def total(rows):
            return S0[dp, rows, :] + RL[dp, rows, :].astype(F32) + RR[dp, rows, :].astype(F32)
        if dp == 2:
            bF[lo, :] = total(lo).astype(BF16)
            go(b_far_r)
            bF[hi, :] = total(hi).astype(BF16)
            go(b_far_l)
        elif dp == 1:
            bR[hi, :] = total(hi).astype(BF16)
            go(b_near_r[1])
            T1[...] = total(lo)
        elif dp == 3:
            bL[lo, :] = total(lo).astype(BF16)
            go(b_near_l[0])
            T3[...] = total(hi)
        else:
            T0[lo, :] = total(lo)
            T0[hi, :] = total(hi)

    sg_cp.wait()
    for k, dp in enumerate(order):
        h_cp[dp].wait()
        if k == 0:
            for g in range(4):
                for cp in w_cp[g]:
                    cp.wait()
                down(dp, g * gs, (g + 1) * gs)
        else:
            down(dp, 0, el)
        if k >= 1:
            pass_on(order[k - 1])
        if k >= 2:
            finish(order[k - 2])
        combine(dp, 2, put_far(dp))
        go(far_r[dp], far_l[dp])
        combine(dp, 1, put_right(dp))
        go(near_r[dp][1])
        combine(dp, 3, put_left(dp))
        go(near_l[dp][0])
        combine(dp, 0, put_own(dp))
    pass_on(0)
    b_far_r.wait_recv()
    bR[lo, :] = (T1[...] + bFR[...].astype(F32)).astype(BF16)
    go(b_near_r[0])
    finish(3)
    b_far_l.wait_recv()
    bL[hi, :] = (T3[...] + bFL[...].astype(F32)).astype(BF16)
    go(b_near_l[1])
    finish(0)
    for cp in b_near_r + b_near_l:
        cp.wait_recv()
    o_ref[...] = (T0[...] + bRL[...].astype(F32) + bRR[...].astype(F32)).astype(BF16)
    for cp in sent:
        cp.wait_send()


def _local(mesh, x, idx, g, w1, w3, w2):
    t_loc, d = x.shape
    top = idx.shape[1]
    el, _, fw = w1.shape
    n_exp = el * mesh.shape["ep"]
    cap = CF * top * t_loc // n_exp
    hf = t_loc // 2
    meta = jnp.concatenate([idx.T.astype(F32), g.T], axis=0)
    hbm = pl.BlockSpec(memory_space=pl.ANY)
    vmem = pl.BlockSpec(memory_space=pltpu.VMEM)
    sems = pltpu.SemaphoreType.DMA
    h, sg, w2x = pl.pallas_call(
        functools.partial(_up, cap),
        out_shape=(jax.ShapeDtypeStruct((4, el, 4 * cap, 2 * fw), BF16),
                   jax.ShapeDtypeStruct((16, 2 * el, t_loc), F32),
                   jax.ShapeDtypeStruct(w2.shape, BF16)),
        in_specs=[hbm] * 5,
        out_specs=(hbm, hbm, hbm),
        scratch_shapes=[
            pltpu.VMEM((4, 4, t_loc, d), BF16),
            pltpu.VMEM((4, 4, 2 * top, t_loc), F32),
            pltpu.VMEM((el, 2, d, 2 * fw), BF16),
            pltpu.VMEM((el, 4 * cap, d), BF16),
            pltpu.VMEM((4, el, 4 * cap, 2 * fw), BF16),
            pltpu.VMEM((16, 2 * el, t_loc), F32),
            sems((40,)), sems((40,)), sems((16,)),
        ],
        compiler_params=pltpu.CompilerParams(collective_id=0, has_side_effects=True, vmem_limit_bytes=VMEM_LIMIT),
    )(x, meta, w1, w3, w2)
    half, full = (hf, d), (t_loc, d)
    return pl.pallas_call(
        functools.partial(_down, cap),
        out_shape=jax.ShapeDtypeStruct((t_loc, d), BF16),
        in_specs=[hbm] * 4,
        out_specs=vmem,
        scratch_shapes=[
            pltpu.VMEM((el, 2 * fw, d), BF16),
            pltpu.VMEM((4, el, 4 * cap, 2 * fw), BF16),
            pltpu.VMEM((4, el * cap, d), BF16),
            pltpu.VMEM((16, 2 * el, t_loc), F32),
            pltpu.VMEM((3 * t_loc, el * cap), BF16),
            pltpu.VMEM((4,) + full, BF16), pltpu.VMEM((4,) + full, BF16), pltpu.VMEM((4,) + full, BF16),
            pltpu.VMEM((4,) + full, F32), pltpu.VMEM((4,) + half, F32), pltpu.VMEM((4,) + half, F32),
            pltpu.VMEM((4,) + half, BF16), pltpu.VMEM((4,) + half, BF16),
            pltpu.VMEM((4,) + full, BF16), pltpu.VMEM((4,) + full, BF16),
            pltpu.VMEM(full, BF16), pltpu.VMEM(full, BF16), pltpu.VMEM(full, BF16),
            pltpu.VMEM(full, F32), pltpu.VMEM(half, F32), pltpu.VMEM(half, F32),
            pltpu.VMEM(half, BF16), pltpu.VMEM(half, BF16), pltpu.VMEM(full, BF16), pltpu.VMEM(full, BF16),
            sems((40,)), sems((40,)), sems((16,)),
        ],
        compiler_params=pltpu.CompilerParams(collective_id=1, has_side_effects=True, vmem_limit_bytes=VMEM_LIMIT),
    )(h, sg, w2, w2x)


def solution(mesh):
    rows = P(("dp", "ep", "tp"), None)
    return jax.shard_map(functools.partial(_local, mesh), mesh=mesh,
                         in_specs=(rows, rows, rows, P("ep", None, "tp"), P("ep", None, "tp"), P("ep", "tp", None)),
                         out_specs=rows, check_vma=False)
```

time: 1520 us -> 127 us (0.08)
  blocking collectives: 844 us -> 0 us
  waiting for transfers between devices: 388 us -> 0 us
  Pallas kernels: 0 us -> 123 us
  local copies, waits for them, and re-layouts: 123 us -> 1.88 us
  matrix products: 91.8 us -> 0 us
  other arithmetic: 52.8 us -> 1.97 us
    all_to_all x2 -> x0, blocking collectives: 844 us -> none  [the longest x1 741 us: local(): parts = lax.all_to_all(yp, 'tp', 0, 0, tiled=True)]
    all_gather x1 -> x0, waiting for transfers between devices: 296 us -> none  [local(): allr = lax.all_gather(recv, 'tp', axis=0)]
    pallas_call x0 -> x2, Pallas kernels: none -> 123 us  [the longest x1 66.4 us: _local(): pl.pallas_call(functools.partial(_up, cap), out_shape=(jax.ShapeDtypeStru...]
    all_to_all x1 -> x0, waiting for transfers between devices: 92.3 us -> none  [local(): back = lax.all_to_all(y, 'ep', 0, 0, tiled=True).reshape(n_exp * cap, d)]
    dot_general x2 -> x0, matrix products: 91.8 us -> none  [the longest x1 60.9 us: local(): jnp.einsum('erf,efd->erd', h, w2, preferred_element_type=jnp.float32)]
    all_gather x1 -> x0, local copies, waits for them, and re-layouts: 44.1 us -> none  [local(): allr = lax.all_gather(recv, 'tp', axis=0)]
    reshape x1 -> x0, local copies, waits for them, and re-layouts: 44.1 us -> none  [local(): yp = yp.reshape(el, tp, ep, cap, d).transpose(1, 2, 0, 3, 4)]
    reduce_sum x3 -> x0, other arithmetic: 33.3 us -> none  [the longest x1 25.9 us: local(): y = jnp.sum(parts.astype(jnp.float32), axis=0).astype(jnp.bfloat16)]
  transfers between devices with their start and end apart: 2 -> 0, of which waited for: 2 -> 0; matrix products, arithmetic and copies ran while one was open for 0% -> 0% of each run, Pallas kernels for 0% -> 0%
where the time goes in v1:
time: 127 us
  Pallas kernels  123 us (97%)
  other arithmetic  1.97 us (2%)
  local copies, waits for them, and re-layouts  1.88 us (1%)
    pallas_call x1, Pallas kernels, _local(): pl.pallas_call(functools.partial(_up, cap), out_shape=(jax.ShapeDtypeStru...  66.4 us
    pallas_call x1, Pallas kernels, _local(): pl.pallas_call(functools.partial(_down, cap), out_shape=jax.ShapeDtypeStr...  56.6 us

profile of v1, /device:TPU:97, one launch (start us, length us, event | category | flops | bytes accessed | tf_op | source)
XLA Modules:
  0.0 126.8 jit_solution(1953460290932531183)
XLA Ops:
  0.0 0.7 convert_bitcast_fusion
  0.7 1.3 %pad_maximum_fusion.meta = f32[16,128]{1,0:T(8,128)} fusion(f32[8,128]{1,0:T(8,128)} %bitcast.3, f32[8,128]{1,0:T(8,128)S(1)} %convert_bitcast_fusion), kind=kLoop, calls=%fused_computation | loop fusion | flops 2048 | bytes 16384 | tf_op jit(solution)/shard_map/concatenate | solution.py:395
  2.0 66.4 %shard_map.64 = (bf16[4,16,128,256]{3,2,1,0:T(8,128)(2,1)}, f32[16,32,128]{2,1,0:T(8,128)}, bf16[16,128,2048]{2,1,0:T(8,128)(2,1)}) custom-call(bf16[128,2048]{1,0:T(8,128)(2,1)} %x.1, f32[16,128]{1,0:T(8,128)} %pad_maximum_fusion.meta, bf16[16,2048,128]{2,1,0:T(8,128)(2,1)} %w1.1, bf16[16,2048,128]{2,1,0:T(8,128)(2,1)} %w3.1, bf16[16,128,2048]{2,1,0:T(8,128)(2,1)} %w2.3), custom_call_target="tpu_custom_call" | custom-call | tf_op jit(solution)/shard_map/pallas_call | solution.py:399
  68.4 56.6 %shard_map.65 = bf16[128,2048]{1,0:T(8,128)(2,1)} custom-call(bf16[4,16,128,256]{3,2,1,0:T(8,128)(2,1)} %get-tuple-element.8.h_in, f32[16,32,128]{2,1,0:T(8,128)} %get-tuple-element.9.sg_in, bf16[16,128,2048]{2,1,0:T(8,128)(2,1)} %w2.3, bf16[16,128,2048]{2,1,0:T(8,128)(2,1)} %get-tuple-element.10.w2x), custom_call_target="tpu_custom_call" | custom-call | tf_op jit(solution)/shard_map/pallas_call | solution.py:418
  124.9 1.9 %copy.8 = bf16[128,2048]{1,0:T(8,128)(2,1)} copy(bf16[128,2048]{1,0:T(8,128)(2,1)} %shard_map.65) | data formatting | bytes 1048576

commit v2 on v0

v2 whole, which is shorter than its diff:
```python
import functools

import jax
import jax.numpy as jnp
from jax import lax
from jax.experimental import pallas as pl
from jax.experimental.pallas import tpu as pltpu
from jax.sharding import PartitionSpec as P

CF = 2
RING = 4
MESH = pl.DeviceIdType.MESH
F32, BF16 = jnp.float32, jnp.bfloat16
VMEM_LIMIT = 67043328
GATHER_UNROLL = 2
UP_UNROLL = 8


def _neighbours():
    d, y, t = lax.axis_index("dp"), lax.axis_index("ep"), lax.axis_index("tp")
    x, c = t // 2, t % 2

    def at(dx, dy):
        return (d, (y + dy) % RING, 2 * ((x + dx) % RING) + c)

    pr, pl_ = at(1 - c, c), at(RING - 1 + c, RING - c)
    qr, ql = at(c, 1 - c), at(RING - c, RING - 1 + c)
    return pr, pl_, qr, ql, (d, y, 2 * x + 1 - c)


def _greet(devices):
    barrier = pltpu.get_barrier_semaphore()
    for dev in devices:
        pl.semaphore_signal(barrier, inc=1, device_id=dev, device_id_type=MESH)
    pl.semaphore_wait(barrier, len(devices))


def _layer(cap, x, idx, gate_in, w1, w3, w2, o_out, w2x, A, MA, Wt, G, Hb, SG, C3, FR, FL, RL, RR, bFR, bFL, bRL, bRR,
           ssem, rsem, lsem):
    pr, pl_, qr, ql, mate = _neighbours()
    el, _, fw = w1.shape
    t_loc, d = x.shape
    top = idx.shape[0]
    hf = t_loc // 2
    lo, hi = pl.ds(0, hf), pl.ds(hf, hf)
    gs = el // 4
    count, lcount = [0], [0]
    open_sends = []

    def remote(src, dst, dev):
        i = count[0]
        count[0] += 1
        return pltpu.make_async_remote_copy(src_ref=src, dst_ref=dst, send_sem=ssem.at[i], recv_sem=rsem.at[i],
                                            device_id=dev, device_id_type=MESH)

    def go(*copies):
        for cp in copies:
            cp.start()
            open_sends.append(cp)

    def sent(*copies):
        for cp in copies:
            cp.wait_send()
            open_sends[:] = [o for o in open_sends if o is not cp]

    def local(src, dst):
        i = lcount[0]
        lcount[0] += 1
        cp = pltpu.make_async_copy(src, dst, lsem.at[i])
        cp.start()
        return cp

    own_x = local(x, A.at[0, 0])
    own_w = []
    for g in range(4):
        es = pl.ds(g * gs, gs)
        own_w.append((local(w1.at[es], Wt.at[es, 0, :, pl.ds(0, fw)]), local(w3.at[es], Wt.at[es, 0, :, pl.ds(fw, fw)])))
    MA[0, 0, 0:top, :] = idx[...].astype(F32)
    MA[0, 0, top:2 * top, :] = gate_in[...]
    _greet((pr, pl_, qr, ql, mate))

    r_lo, r_hi = remote(x.at[lo], A.at[0, 3, lo], pr), remote(x.at[hi], A.at[0, 3, hi], pr)
    l_hi, l_lo = remote(x.at[hi], A.at[0, 1, hi], pl_), remote(x.at[lo], A.at[0, 1, lo], pl_)
    r_m, l_m = remote(MA.at[0, 0], MA.at[0, 3], pr), remote(MA.at[0, 0], MA.at[0, 1], pl_)
    go(r_lo, l_hi, r_m, l_m, r_hi, l_lo)
    mate_w = []
    for g in range(4):
        es = pl.ds(g * gs, gs)
        pair = (remote(w1.at[es], Wt.at[es, 1, :, pl.ds(0, fw)], mate), remote(w3.at[es], Wt.at[es, 1, :, pl.ds(fw, fw)], mate))
        go(*pair)
        mate_w.append(pair)
    w2_cp = remote(w2, w2x, mate)
    go(w2_cp)

    f_lo, f_hi = remote(A.at[0, 3, lo], A.at[0, 2, lo], pr), remote(A.at[0, 1, hi], A.at[0, 2, hi], pl_)
    f_m = remote(MA.at[0, 3], MA.at[0, 2], pr)
    r_lo.wait_recv()
    go(f_lo)
    l_hi.wait_recv()
    go(f_hi)
    r_m.wait_recv()
    go(f_m)

    qR = [remote(x if i == 0 else A.at[0, i], A.at[3, i], qr) for i in range(4)]
    qL = [remote(x if i == 0 else A.at[0, i], A.at[1, i], ql) for i in range(4)]
    fR = [remote(A.at[3, i, lo], A.at[2, i, lo], qr) for i in range(4)]
    fL = [remote(A.at[1, i, hi], A.at[2, i, hi], ql) for i in range(4)]
    mR, mL, mF = remote(MA.at[0], MA.at[3], qr), remote(MA.at[0], MA.at[1], ql), remote(MA.at[3], MA.at[2], qr)

    go(qR[0], qL[0])
    l_m.wait_recv()
    l_lo.wait_recv()
    go(qR[1], qL[1])
    r_hi.wait_recv()
    go(qR[3], qL[3])
    f_m.wait_recv()
    go(mR, mL)
    f_lo.wait_recv()
    f_hi.wait_recv()
    go(qR[2], qL[2])
    own_x.wait()

    far_r = [remote(A.at[2, i, lo], FR.at[i], qr) for i in range(4)]
    far_l = [remote(A.at[2, i, hi], FL.at[i], ql) for i in range(4)]
    near_r = [(remote(A.at[1, i, lo], RL.at[i, lo], qr), remote(A.at[1, i, hi], RL.at[i, hi], qr)) for i in range(4)]
    near_l = [(remote(A.at[3, i, lo], RR.at[i, lo], ql), remote(A.at[3, i, hi], RR.at[i, hi], ql)) for i in range(4)]
    b_far_r, b_far_l = remote(A.at[0, 2, lo], bFR, pr), remote(A.at[0, 2, hi], bFL, pl_)
    b_near_r = (remote(A.at[0, 1, lo], bRL.at[lo], pr), remote(A.at[0, 1, hi], bRL.at[hi], pr))
    b_near_l = (remote(A.at[0, 3, lo], bRR.at[lo], pl_), remote(A.at[0, 3, hi], bRR.at[hi], pl_))

    first = (lax.axis_index("ep") * el).astype(F32)
    eid = lax.broadcasted_iota(jnp.int32, (el, t_loc), 0).astype(F32) + first
    tri = (lax.broadcasted_iota(jnp.int32, (t_loc, t_loc), 0)
           < lax.broadcasted_iota(jnp.int32, (t_loc, t_loc), 1)).astype(F32).astype(BF16)
    slot_no = lax.broadcasted_iota(jnp.int32, (cap, t_loc), 0).astype(F32)
    ncol = el * cap
    row_no = lax.broadcasted_iota(jnp.int32, (4 * el, ncol), 0)
    col_e = lax.broadcasted_iota(jnp.int32, (4 * el, ncol), 1) // cap
    spread = [jnp.where(row_no == col_e + k * el, 1.0, 0.0).astype(BF16) for k in range(4)]
    col_s = (lax.broadcasted_iota(jnp.int32, (t_loc, ncol), 1) % cap).astype(F32)

    def gather(block, i0=0, i1=4):
        def one(i):
            b = block(i)
            m = MA.at[b // 4, b % 4]
            hold = jnp.zeros((el, t_loc), F32)
            gate = jnp.zeros((el, t_loc), F32)
            for j in range(top):
                hit = jnp.broadcast_to(m[j:j + 1, :], (el, t_loc)) == eid
                hold = hold + jnp.where(hit, 1.0, 0.0)
                gate = gate + jnp.where(hit, jnp.broadcast_to(m[top + j:top + j + 1, :], (el, t_loc)), 0.0)
            slot = jnp.dot(hold.astype(BF16), tri, preferred_element_type=F32)
            keep = (hold > 0.5) & (slot < cap)
            slot = jnp.where(keep, slot, -1.0)
            SG[b, 0:el, :] = slot
            SG[b, el:2 * el, :] = jnp.where(keep, gate, 0.0)
            pick = jnp.concatenate(
                [jnp.where(jnp.broadcast_to(slot[e:e + 1, :], (cap, t_loc)) == slot_no, 1.0, 0.0) for e in range(el)], axis=0
            ).astype(BF16)
            at = pl.ds(pl.multiple_of(i * cap, cap), cap)
            for n in range(d // 256):
                cols = pl.ds(n * 256, 256)
                rows = jnp.dot(pick, A[b // 4, b % 4, :, cols], preferred_element_type=F32).astype(BF16)
                G[:, at, cols] = rows.reshape(el, cap, 256)

        def body(k, _):
            for u in range(GATHER_UNROLL):
                one(k * GATHER_UNROLL + u)
            return 0
        lax.fori_loop(i0 // GATHER_UNROLL, i1 // GATHER_UNROLL, body, 0)

    def up(e0, n, s, hs, unroll):
        def one(e):
            o = jnp.dot(G[e], Wt[e, s], preferred_element_type=F32)
            Hb[hs, e, :, s * fw:(s + 1) * fw] = (jax.nn.silu(o[:, :fw]) * o[:, fw:]).astype(BF16)

        def body(k, _):
            for u in range(unroll):
                one(e0 + k * unroll + u)
            return 0
        lax.fori_loop(0, n // unroll, body, 0)

    def w2_over(g):
        copies = []
        es = pl.ds(g * gs, gs)
        for n in range(d // 256):
            cols = pl.ds(n * 256, 256)
            copies.append(local(w2.at[es, :, cols], Wt.at[es, 0, pl.ds(n * 256, fw), :]))
            copies.append(local(w2x.at[es, :, cols], Wt.at[es, 0, pl.ds(n * 256 + fw, fw), :]))
        return copies

    def down(hs, k0, k1):
        def body(k, _):
            for u in range(4):
                e = k * 4 + u
                for n in range(d // 256):
                    cols = pl.ds(n * 256, 256)
                    y = jnp.dot(Hb[hs, e], Wt[e, 0, cols, :], preferred_element_type=F32).astype(BF16)
                    for i in range(4):
                        G[4 * i + k, u * cap:(u + 1) * cap, cols] = y[i * cap:(i + 1) * cap]
            return 0
        lax.fori_loop(k0, k1, body, 0)

    def combine(i, dq, dp):
        b = dq * 4 + dp
        gate = SG[b, el:2 * el, :]
        g1 = gate.astype(BF16).astype(F32)
        g2 = (gate - g1).astype(BF16).astype(F32)
        g3 = gate - g1 - g2
        table = jnp.concatenate([SG[b, 0:el, :], g1, g2, g3], axis=0).T.astype(BF16)
        slot = jnp.dot(table, spread[0], preferred_element_type=F32)
        hit = slot == col_s
        for k in range(3):
            piece = jnp.dot(table, spread[k + 1], preferred_element_type=F32)
            C3[k * t_loc:(k + 1) * t_loc, :] = jnp.where(hit, piece, 0.0).astype(BF16)
        for n in range(d // 256):
            cols = pl.ds(n * 256, 256)
            z = jnp.dot(C3[...], G[pl.ds(4 * i, 4), :, cols].reshape(ncol, 256), preferred_element_type=F32)
            A[dq, dp, :, cols] = (z[:t_loc] + z[t_loc:2 * t_loc] + z[2 * t_loc:]).astype(BF16)

    def pass_on(dp):
        far_r[dp].wait_recv()
        A[1, dp, lo, :] = (A[1, dp, lo, :].astype(F32) + FR[dp].astype(F32)).astype(BF16)
        go(near_r[dp][0])
        far_l[dp].wait_recv()
        A[3, dp, hi, :] = (A[3, dp, hi, :].astype(F32) + FL[dp].astype(F32)).astype(BF16)
        go(near_l[dp][1])

    def total(dp, rows):
        return A[0, dp, rows, :].astype(F32) + RL[dp, rows, :].astype(F32) + RR[dp, rows, :].astype(F32)

    gather(lambda i: i)
    for g in range(4):
        for cp in own_w[g]:
            cp.wait()
    up(0, el, 0, 0, UP_UNROLL)
    for g in range(4):
        for cp in mate_w[g]:
            cp.wait_recv()
        up(g * gs, gs, 1, 0, gs)

    mR.wait_recv()
    go(mF)
    mL.wait_recv()
    for i in (0, 1):
        qR[i].wait_recv()
        qL[i].wait_recv()
        go(fR[i], fL[i])
    gather(lambda i: 12 - 8 * (i // 2) + i % 2)
    up(0, el, 0, 1, UP_UNROLL)
    up(0, el, 1, 1, UP_UNROLL)

    for i in (3, 2):
        qR[i].wait_recv()
        qL[i].wait_recv()
        go(fR[i], fL[i])
    gather(lambda i: 14 - 8 * (i // 2) + i % 2)
    up(0, el, 0, 2, UP_UNROLL)
    up(0, el, 1, 2, UP_UNROLL)

    mF.wait_recv()
    for i in (0, 1):
        fR[i].wait_recv()
        fL[i].wait_recv()
    gather(lambda i: 8 + i, 0, 2)
    for i in (3, 2):
        fR[i].wait_recv()
        fL[i].wait_recv()
    gather(lambda i: 8 + i, 2, 4)
    w2_cp.wait_recv()
    w2_cps = []
    for g in range(2):
        up(2 * g * gs, 2 * gs, 0, 3, UP_UNROLL)
        w2_cps += [w2_over(2 * g), w2_over(2 * g + 1)]
    up(0, el, 1, 3, UP_UNROLL)
    for k in range(4):
        for cp in w2_cps[k]:
            cp.wait()
        down(3, k, k + 1)
    for dp in (2, 1, 3, 0):
        combine(dp, 2, dp)
        go(far_r[dp], far_l[dp])

    down(2, 0, 4)
    sent(fR[2], fL[2], fR[3], fL[3])
    for i, dp in ((0, 2), (1, 3)):
        combine(i, 3, dp)
        go(near_l[dp][0])
        combine(i + 2, 1, dp)
        go(near_r[dp][1])
    pass_on(2)
    pass_on(3)
    down(1, 0, 4)
    sent(fR[0], fL[0], fR[1], fL[1])

    def chunk1(i, _):
        combine(i, 3, i)
        combine(i + 2, 1, i)
        return 0
    lax.fori_loop(0, 2, chunk1, 0)
    for dp in (1, 0):
        go(near_l[dp][0], near_r[dp][1])
        pass_on(dp)

    down(0, 0, 4)
    sent(*qR, *qL, f_lo, f_hi)
    combine(2, 0, 2)
    for cp in near_r[2] + near_l[2]:
        cp.wait_recv()
    A[0, 2, lo, :] = total(2, lo).astype(BF16)
    go(b_far_r)
    A[0, 2, hi, :] = total(2, hi).astype(BF16)
    go(b_far_l)

    def chunk0(k, _):
        dp = (2 * k + 1) % 5
        combine(dp, 0, dp)
        return 0
    lax.fori_loop(0, 3, chunk0, 0)
    for cp in near_r[1] + near_l[1]:
        cp.wait_recv()
    A[0, 1, hi, :] = total(1, hi).astype(BF16)
    go(b_near_r[1])
    for cp in near_r[3] + near_l[3]:
        cp.wait_recv()
    A[0, 3, lo, :] = total(3, lo).astype(BF16)
    go(b_near_l[0])
    b_far_r.wait_recv()
    A[0, 1, lo, :] = (total(1, lo) + bFR[...].astype(F32)).astype(BF16)
    go(b_near_r[0])
    b_far_l.wait_recv()
    A[0, 3, hi, :] = (total(3, hi) + bFL[...].astype(F32)).astype(BF16)
    go(b_near_l[1])
    for cp in near_r[0] + near_l[0] + b_near_r + b_near_l:
        cp.wait_recv()
    for rows in (lo, hi):
        A[0, 0, rows, :] = (total(0, rows) + bRL[rows, :].astype(F32) + bRR[rows, :].astype(F32)).astype(BF16)
    out_cp = local(A.at[0, 0], o_out)
    for cp in open_sends:
        cp.wait_send()
    out_cp.wait()


def _local(mesh, x, idx, g, w1, w3, w2):
    t_loc, d = x.shape
    top = idx.shape[1]
    el, _, fw = w1.shape
    cap = CF * top * t_loc // (el * mesh.shape["ep"])
    half, full = (t_loc // 2, d), (t_loc, d)
    hbm = pl.BlockSpec(memory_space=pl.ANY)
    vmem = pl.BlockSpec(memory_space=pltpu.VMEM)
    sems = pltpu.SemaphoreType.DMA
    out, _ = pl.pallas_call(
        functools.partial(_layer, cap),
        out_shape=(jax.ShapeDtypeStruct((t_loc, d), BF16), jax.ShapeDtypeStruct(w2.shape, BF16)),
        in_specs=[hbm, vmem, vmem, hbm, hbm, hbm],
        out_specs=(hbm, hbm),
        scratch_shapes=[
            pltpu.VMEM((4, 4) + full, BF16),
            pltpu.VMEM((4, 4, 2 * top, t_loc), F32),
            pltpu.VMEM((el, 2, d, 2 * fw), BF16),
            pltpu.VMEM((el, 4 * cap, d), BF16),
            pltpu.VMEM((4, el, 4 * cap, 2 * fw), BF16),
            pltpu.VMEM((16, 2 * el, t_loc), F32),
            pltpu.VMEM((3 * t_loc, el * cap), BF16),
            pltpu.VMEM((4,) + half, BF16), pltpu.VMEM((4,) + half, BF16),
            pltpu.VMEM((4,) + full, BF16), pltpu.VMEM((4,) + full, BF16),
            pltpu.VMEM(half, BF16), pltpu.VMEM(half, BF16), pltpu.VMEM(full, BF16), pltpu.VMEM(full, BF16),
            sems((80,)), sems((80,)), sems((80,)),
        ],
        compiler_params=pltpu.CompilerParams(collective_id=0, has_side_effects=True, vmem_limit_bytes=VMEM_LIMIT),
    )(x, idx.T, g.T, w1, w3, w2)
    return out


def solution(mesh):
    rows = P(("dp", "ep", "tp"), None)
    return jax.shard_map(functools.partial(_local, mesh), mesh=mesh,
                         in_specs=(rows, rows, rows, P("ep", None, "tp"), P("ep", None, "tp"), P("ep", "tp", None)),
                         out_specs=rows, check_vma=False)
```

time: 1520 us -> 115 us (0.08)
  blocking collectives: 844 us -> 0 us
  waiting for transfers between devices: 388 us -> 0 us
  local copies, waits for them, and re-layouts: 123 us -> 1.88 us
  Pallas kernels: 0 us -> 113 us
  matrix products: 91.8 us -> 0 us
  other arithmetic: 52.8 us -> 0 us
    all_to_all x2 -> x0, blocking collectives: 844 us -> none  [the longest x1 741 us: local(): parts = lax.all_to_all(yp, 'tp', 0, 0, tiled=True)]
    all_gather x1 -> x0, waiting for transfers between devices: 296 us -> none  [local(): allr = lax.all_gather(recv, 'tp', axis=0)]
    pallas_call x0 -> x1, Pallas kernels: none -> 113 us  [_local(): pl.pallas_call(functools.partial(_layer, cap), out_shape=(jax.ShapeDtypeS...]
    all_to_all x1 -> x0, waiting for transfers between devices: 92.3 us -> none  [local(): back = lax.all_to_all(y, 'ep', 0, 0, tiled=True).reshape(n_exp * cap, d)]
    dot_general x2 -> x0, matrix products: 91.8 us -> none  [the longest x1 60.9 us: local(): jnp.einsum('erf,efd->erd', h, w2, preferred_element_type=jnp.float32)]
    all_gather x1 -> x0, local copies, waits for them, and re-layouts: 44.1 us -> none  [local(): allr = lax.all_gather(recv, 'tp', axis=0)]
    reshape x1 -> x0, local copies, waits for them, and re-layouts: 44.1 us -> none  [local(): yp = yp.reshape(el, tp, ep, cap, d).transpose(1, 2, 0, 3, 4)]
    reduce_sum x3 -> x0, other arithmetic: 33.3 us -> none  [the longest x1 25.9 us: local(): y = jnp.sum(parts.astype(jnp.float32), axis=0).astype(jnp.bfloat16)]
  transfers between devices with their start and end apart: 2 -> 0, of which waited for: 2 -> 0; matrix products, arithmetic and copies ran while one was open for 0% -> 0% of each run, Pallas kernels for 0% -> 0%
where the time goes in v2:
time: 115 us
  Pallas kernels  113 us (98%)
  local copies, waits for them, and re-layouts  1.88 us (2%)
    pallas_call x1, Pallas kernels, _local(): pl.pallas_call(functools.partial(_layer, cap), out_shape=(jax.ShapeDtypeS...  113 us

profile of v2, /device:TPU:97, one launch (start us, length us, event | category | flops | bytes accessed | tf_op | source)
XLA Modules:
  0.0 114.8 jit_solution(10061195478987758653)
XLA Ops:
  0.0 112.9 %shard_map.64 = (bf16[128,2048]{1,0:T(8,128)(2,1)}, bf16[16,128,2048]{2,1,0:T(8,128)(2,1)}) custom-call(bf16[128,2048]{1,0:T(8,128)(2,1)} %x.1, s32[8,128]{1,0:T(8,128)} %bitcast.2, f32[8,128]{1,0:T(8,128)} %bitcast.3, bf16[16,2048,128]{2,1,0:T(8,128)(2,1)} %w1.1, bf16[16,2048,128]{2,1,0:T(8,128)(2,1)} %w3.1, bf16[16,128,2048]{2,1,0:T(8,128)(2,1)} %w2.1), custom_call_target="tpu_custom_call" | custom-call | tf_op jit(solution)/shard_map/pallas_call | solution.py:353
  113.0 1.9 %copy.8 = bf16[128,2048]{1,0:T(8,128)(2,1)} copy(bf16[128,2048]{1,0:T(8,128)(2,1)} %get-tuple-element.6) | data formatting | bytes 1048576
